TPU v7x, 32 devices: a whole 2x2x4 slice. The times are simulated.
32 devices in a mesh: dp: 4 (over z), feat: 8 (over y, x, core).
Axes of the slice: x: 2, y: 2, z: 4, core: 2. Of those that a mesh axis runs over, the one named last changes fastest.
Arguments:
- features: float32 [4096, 8192], P('dp', 'feat'), may hold values from -0.0625 to 0.0625
- labels: int32 [4096], P('dp'), may hold values from -1 to 1, as said below
- weights: float32 [8192], P('feat'), may hold values from -6 to 6
Outputs:
- gradient: float32 [8192], P('feat')
- newton_step: float32 [8192], P('feat')
- residual: float32 [8192], P('feat')
Inputs may be any that keep to these rules, and one draw needn't show every extreme that they name: `labels`: every label is -1 or +1.
All inputs are finite; a program needn't handle non-finite values.
Results may differ from a plain program's by a relative error of at most 0.0003.
Values sent between devices are 32-bit elements; how exact they have to be, the bound alone decides.
A program may use at most 64 MiB of HBM per device.

v0:
```python
import jax
import jax.numpy as jnp
from jax import lax
from jax.sharding import PartitionSpec as P

CG_STEPS = 3
PENALTY = 4.0
HIGH = lax.Precision.HIGHEST


def squares(residual):
    return lax.psum(jnp.sum(residual * residual), "feat")


def local(features, labels, weights):
    y = labels.astype(jnp.float32)
    margin = y * lax.psum(jnp.dot(features, weights, precision=HIGH), "feat")
    sig = 1.0 / (1.0 + jnp.exp(-margin))
    local_grad = jnp.dot((sig - 1.0) * y, features, precision=HIGH)
    gradient = weights + PENALTY * lax.psum(local_grad, "dp")
    curv = PENALTY * sig * (1.0 - sig)
    newton_step = jnp.zeros_like(weights)
    residual = -gradient
    direction = residual
    rr = squares(residual)
    for step in range(CG_STEPS):
        image_rows, dir_sq = lax.psum(
            (jnp.dot(features, direction, precision=HIGH), jnp.sum(direction * direction)), "feat"
        )
        weighted = curv * image_rows
        back, quad = lax.psum(
            (jnp.dot(weighted, features, precision=HIGH), jnp.sum(weighted * image_rows)), "dp"
        )
        curvature = dir_sq + quad
        image = direction + back
        alpha = rr / curvature
        newton_step = newton_step + alpha * direction
        residual = residual - alpha * image
        fresh = squares(residual)
        direction = residual + fresh / rr * direction
        rr = fresh
    return (gradient, newton_step, residual)


def solution(mesh):
    placed = (P("dp", "feat"), P("dp"), P("feat"))
    return jax.shard_map(
        local,
        mesh=mesh,
        in_specs=placed,
        out_specs=(P("feat"), P("feat"), P("feat")),
        check_vma=False,
    )
```

profile of v0, /device:TPU:0, one launch (start us, length us, event | category | flops | bytes accessed | tf_op | source)
XLA Modules:
  0.0 174.1 jit_solution(13997829717275814949)
XLA Ops:
  0.6 0.0 copy-start.2
  0.6 0.0 copy-start.1
  0.7 5.8 %fusion.3 = f32[1,1024]{1,0:T(1,128)S(1)} fusion(f32[1024,1024]{1,0:T(8,128)} %param.3, f32[1024,1]{0,1:T(1,128)} %bitcast.34), kind=kOutput, calls=%fused_computation.21 | convolution fusion | flops 12582912 | bytes 4202496 | tf_op jit(solution)/shard_map/dot_general | solution.py:17
  6.4 15.2 %psum.115 = f32[1024]{0:T(1024)S(1)} all-reduce(f32[1024]{0:T(1024)S(1)} %bitcast.45), channel_id=1, replica_groups=mesh['dp'=4,'feat'=8] {'feat'}, use_global_device_ids=true, to_apply=%region_0.0 | all-reduce | flops 1024 | bytes 8192 | tf_op jit(solution)/shard_map/psum | solution.py:17
  21.6 0.0 copy-done.2
  21.6 4.3 %fusion.4 = f32[1,1024]{1,0:T(1,128)S(1)} fusion(f32[1024,1]{0,1:T(1,128)S(1)} %bitcast.47, f32[1024,1024]{1,0:T(8,128)} %param.3), kind=kOutput, calls=%fused_computation.22 | convolution fusion | flops 12582912 | bytes 4202496 | tf_op jit(solution)/shard_map/dot_general | solution.py:19
  25.9 11.9 %psum.116 = f32[1024]{0:T(1024)S(1)} all-reduce(f32[1024]{0:T(1024)S(1)} %bitcast.44), channel_id=1, replica_groups=mesh['dp'=4,'feat'=8] {'dp'}, use_global_device_ids=true, to_apply=%region_1.0 | all-reduce | flops 1024 | bytes 8192 | tf_op jit(solution)/shard_map/psum | solution.py:20
  37.8 0.0 copy-done.1
  37.8 0.6 multiply_reduce_fusion.7
  38.4 0.0 copy-start
  38.4 5.6 %fusion.5 = f32[1,1024]{1,0:T(1,128)S(1)} fusion(f32[1024,1]{0,1:T(1,128)S(1)} %bitcast.46, f32[1024,1024]{1,0:T(8,128)} %param.3), kind=kOutput, calls=%fused_computation.23 | convolution fusion | flops 12582912 | bytes 4202496 | tf_op jit(solution)/shard_map/dot_general | solution.py:28
  44.1 12.8 %all-reduce.2 = (f32[1024]{0:T(1024)S(1)}, f32[]{:T(128)}) all-reduce(f32[1024]{0:T(1024)S(1)} %bitcast.38, f32[]{:T(128)} %get-tuple-element.21), channel_id=1, replica_groups=mesh['dp'=4,'feat'=8] {'feat'}, use_global_device_ids=true, to_apply=%region_4.0 | all-reduce | flops 1025 | bytes 8200 | tf_op jit(solution)/shard_map/psum | solution.py:27
  56.8 0.6 multiply_reduce_fusion.6
  57.4 4.3 %fusion.6 = f32[1,1024]{1,0:T(1,128)S(1)} fusion(f32[1024,1]{0,1:T(1,128)S(1)} %bitcast.36, f32[1024,1024]{1,0:T(8,128)} %param.3), kind=kOutput, calls=%fused_computation.24 | convolution fusion | flops 12582912 | bytes 4202496 | tf_op jit(solution)/shard_map/dot_general | solution.py:32
  61.7 9.1 %all-reduce.5 = (f32[1024]{0:T(1024)S(1)}, f32[]{:T(128)}) all-reduce(f32[1024]{0:T(1024)S(1)} %bitcast.39, f32[]{:T(128)} %get-tuple-element.29), channel_id=1, replica_groups=mesh['dp'=4,'feat'=8] {'dp'}, use_global_device_ids=true, to_apply=%region_7.0 | all-reduce | flops 1025 | bytes 8200 | tf_op jit(solution)/shard_map/psum | solution.py:31
  72.7 0.6 multiply_reduce_fusion.5
  73.3 12.6 %psum.121 = f32[]{:T(128)} all-reduce(f32[]{:T(128)} %multiply_reduce_fusion.5), channel_id=1, replica_groups=mesh['dp'=4,'feat'=8] {'feat'}, use_global_device_ids=true, to_apply=%region_9.0 | all-reduce | flops 1 | bytes 8 | tf_op jit(solution)/shard_map/psum | solution.py:12
  87.3 0.6 multiply_reduce_fusion.4
  87.9 5.6 %fusion.7 = f32[1,1024]{1,0:T(1,128)S(1)} fusion(f32[1024,1]{0,1:T(1,128)S(1)} %bitcast.32, f32[1024,1024]{1,0:T(8,128)} %param.3), kind=kOutput, calls=%fused_computation.25 | convolution fusion | flops 12582912 | bytes 4202496 | tf_op jit(solution)/shard_map/dot_general | solution.py:28
  93.5 12.8 %all-reduce.1 = (f32[1024]{0:T(1024)S(1)}, f32[]{:T(128)}) all-reduce(f32[1024]{0:T(1024)S(1)} %bitcast.42, f32[]{:T(128)} %get-tuple-element.19), channel_id=1, replica_groups=mesh['dp'=4,'feat'=8] {'feat'}, use_global_device_ids=true, to_apply=%region_12.0 | all-reduce | flops 1025 | bytes 8200 | tf_op jit(solution)/shard_map/psum | solution.py:27
  106.3 0.7 multiply_reduce_fusion.3
  107.0 4.3 %fusion.8 = f32[1,1024]{1,0:T(1,128)S(1)} fusion(f32[1024,1]{0,1:T(1,128)S(1)} %bitcast.37, f32[1024,1024]{1,0:T(8,128)} %param.3), kind=kOutput, calls=%fused_computation.26 | convolution fusion | flops 12582912 | bytes 4202496 | tf_op jit(solution)/shard_map/dot_general | solution.py:32
  111.2 11.1 %all-reduce.4 = (f32[1024]{0:T(1024)S(1)}, f32[]{:T(128)}) all-reduce(f32[1024]{0:T(1024)S(1)} %bitcast.40, f32[]{:T(128)} %get-tuple-element.27), channel_id=1, replica_groups=mesh['dp'=4,'feat'=8] {'dp'}, use_global_device_ids=true, to_apply=%region_15.0 | all-reduce | flops 1025 | bytes 8200 | tf_op jit(solution)/shard_map/psum | solution.py:31
  124.2 0.6 multiply_reduce_fusion.2
  124.8 12.4 %psum.126 = f32[]{:T(128)} all-reduce(f32[]{:T(128)} %get-tuple-element.17), channel_id=1, replica_groups=mesh['dp'=4,'feat'=8] {'feat'}, use_global_device_ids=true, to_apply=%region_17.0 | all-reduce | flops 1 | bytes 8 | tf_op jit(solution)/shard_map/psum | solution.py:12
  138.6 0.6 multiply_reduce_fusion.1
  139.2 5.6 %fusion.9 = f32[1,1024]{1,0:T(1,128)S(1)} fusion(f32[1024,1]{0,1:T(1,128)S(1)} %bitcast.33, f32[1024,1024]{1,0:T(8,128)} %param.3), kind=kOutput, calls=%fused_computation.27 | convolution fusion | flops 12582912 | bytes 4202496 | tf_op jit(solution)/shard_map/dot_general | solution.py:28
  144.8 12.7 %all-reduce = (f32[]{:T(128)}, f32[1024]{0:T(1024)S(1)}) all-reduce(f32[]{:T(128)} %get-tuple-element.15, f32[1024]{0:T(1024)S(1)} %bitcast.43), channel_id=1, replica_groups=mesh['dp'=4,'feat'=8] {'feat'}, use_global_device_ids=true, to_apply=%region_19.0 | all-reduce | flops 1025 | bytes 8200 | tf_op jit(solution)/shard_map/psum | solution.py:27
  157.6 0.7 fusion
  158.3 4.3 %fusion.10 = f32[1,1024]{1,0:T(1,128)S(1)} fusion(f32[1024,1]{0,1:T(1,128)S(1)} %bitcast.35, f32[1024,1024]{1,0:T(8,128)} %param.3), kind=kOutput, calls=%fused_computation.28 | convolution fusion | flops 12582912 | bytes 4202496 | tf_op jit(solution)/shard_map/dot_general | solution.py:32
  162.5 9.1 %all-reduce.3 = (f32[]{:T(128)}, f32[1024]{0:T(1024)S(1)}) all-reduce(f32[]{:T(128)} %get-tuple-element.26, f32[1024]{0:T(1024)S(1)} %bitcast.41), channel_id=1, replica_groups=mesh['dp'=4,'feat'=8] {'dp'}, use_global_device_ids=true, to_apply=%region_22.0 | all-reduce | flops 1025 | bytes 8200 | tf_op jit(solution)/shard_map/psum | solution.py:31
  173.5 0.0 copy-done
  173.5 0.6 multiply_subtract_fusion
  (2 shorter events, 0.0 us)
Async XLA Ops:
  0.6 20.9 %copy-start.2 = (s32[1024]{0:T(1024)S(1)}, s32[1024]{0:T(1024)}, u32[]{:S(2)}) copy-start(s32[1024]{0:T(1024)} %param.4) | copy-start | bytes 12292
  0.6 37.2 %copy-start.1 = (f32[1024]{0:T(1024)S(1)}, f32[1024]{0:T(1024)}, u32[]{:S(2)}) copy-start(f32[1024]{0:T(1024)} %param.5) | copy-start | bytes 12292
  38.4 135.1 %copy-start = (f32[1024]{0:T(1024)}, f32[1024]{0:T(1024)S(1)}, u32[]{:S(2)}) copy-start(f32[1024]{0:T(1024)S(1)} %get-tuple-element.22) | copy-start | bytes 12292
where the time goes:
time: 175 us; the launch traced here: 174 us
  blocking collectives  120 us (69%)
  matrix products  39.8 us (23%)
  between operations  9.03 us (5%)
  other arithmetic  5.6 us (3%)
    psum x3, blocking collectives, local(): lax.psum((jnp.dot(features, direction, precision=HIGH), jnp.sum(direction...  38.2 us
    psum x3, blocking collectives, local(): lax.psum((jnp.dot(weighted, features, precision=HIGH), jnp.sum(weighted *...  29.4 us
    psum x2, blocking collectives, squares(): return lax.psum(jnp.sum(residual * residual), 'feat')  25 us
    dot_general x3, matrix products, local(): jnp.dot(features, direction, precision=HIGH)  16.9 us
    psum x1, blocking collectives, local(): margin = y * lax.psum(jnp.dot(features, weights, precision=HIGH), 'feat')  15.2 us
    dot_general x3, matrix products, local(): jnp.dot(weighted, features, precision=HIGH)  12.8 us
    psum x1, blocking collectives, local(): gradient = weights + PENALTY * lax.psum(local_grad, 'dp')  11.9 us
    dot_general x1, matrix products, local(): margin = y * lax.psum(jnp.dot(features, weights, precision=HIGH), 'feat')  5.76 us

commit v1 on v0

--- a/solution.py
+++ b/solution.py
@@ -17,7 +17,7 @@
     margin = y * lax.psum(jnp.dot(features, weights, precision=HIGH), "feat")
     sig = 1.0 / (1.0 + jnp.exp(-margin))
     local_grad = jnp.dot((sig - 1.0) * y, features, precision=HIGH)
-    gradient = weights + PENALTY * lax.psum(local_grad, "dp")
+    gradient = weights + PENALTY * jnp.sum(lax.all_gather(local_grad, "dp"), axis=0)
     curv = PENALTY * sig * (1.0 - sig)
     newton_step = jnp.zeros_like(weights)
     residual = -gradient

time: 175 us -> 180 us (1.029)
  blocking collectives: 120 us -> 125 us
    all_gather x0 -> x1, blocking collectives: none -> 13.4 us  [local(): lax.all_gather(local_grad, 'dp')]
    psum x1 -> x0, blocking collectives: 11.9 us -> none  [local(): gradient = weights + PENALTY * lax.psum(local_grad, 'dp')]
    psum x3, blocking collectives: 29.4 us -> 32.8 us  [local(): lax.psum((jnp.dot(weighted, features, precision=HIGH), jnp.sum(weighted *...]
where the time goes in v1:
time: 180 us; the launch traced here: 179 us
  blocking collectives  125 us (69%)
  matrix products  39.8 us (22%)
  between operations  9.04 us (5%)
  other arithmetic  5.62 us (3%)
    psum x3, blocking collectives, local(): lax.psum((jnp.dot(features, direction, precision=HIGH), jnp.sum(direction...  38.2 us
    psum x3, blocking collectives, local(): lax.psum((jnp.dot(weighted, features, precision=HIGH), jnp.sum(weighted *...  32.8 us
    psum x2, blocking collectives, squares(): return lax.psum(jnp.sum(residual * residual), 'feat')  25 us
    dot_general x3, matrix products, local(): jnp.dot(features, direction, precision=HIGH)  16.9 us
    psum x1, blocking collectives, local(): margin = y * lax.psum(jnp.dot(features, weights, precision=HIGH), 'feat')  15.2 us
    all_gather x1, blocking collectives, local(): lax.all_gather(local_grad, 'dp')  13.4 us
    dot_general x3, matrix products, local(): jnp.dot(weighted, features, precision=HIGH)  12.8 us
    dot_general x1, matrix products, local(): margin = y * lax.psum(jnp.dot(features, weights, precision=HIGH), 'feat')  5.76 us

profile of v1, /device:TPU:0, one launch (start us, length us, event | category | flops | bytes accessed | tf_op | source)
XLA Modules:
  0.0 179.1 jit_solution(14512712680258148531)
XLA Ops:
  0.6 0.0 copy-start.2
  0.6 0.0 copy-start.1
  0.7 5.8 %fusion.3 = f32[1,1024]{1,0:T(1,128)S(1)} fusion(f32[1024,1024]{1,0:T(8,128)} %param.3, f32[1024,1]{0,1:T(1,128)} %bitcast.34), kind=kOutput, calls=%fused_computation.21 | convolution fusion | flops 12582912 | bytes 4202496 | tf_op jit(solution)/shard_map/dot_general | solution.py:17
  6.4 15.2 %psum.108 = f32[1024]{0:T(1024)S(1)} all-reduce(f32[1024]{0:T(1024)S(1)} %bitcast.45), channel_id=1, replica_groups=mesh['dp'=4,'feat'=8] {'feat'}, use_global_device_ids=true, to_apply=%region_0.0 | all-reduce | flops 1024 | bytes 8192 | tf_op jit(solution)/shard_map/psum | solution.py:17
  21.6 0.0 copy-done.2
  21.6 4.3 %fusion.4 = f32[1,1024]{1,0:T(1,128)S(1)} fusion(f32[1024,1]{0,1:T(1,128)S(1)} %bitcast.47, f32[1024,1024]{1,0:T(8,128)} %param.3), kind=kOutput, calls=%fused_computation.22 | convolution fusion | flops 12582912 | bytes 4202496 | tf_op jit(solution)/shard_map/dot_general | solution.py:19
  25.9 13.4 %all-gather = f32[4096]{0:T(1024)S(1)} all-gather(f32[1024]{0:T(1024)S(1)} %bitcast.38), channel_id=2, replica_groups=mesh['dp'=4,'feat'=8] {'dp'}, dimensions={0}, use_global_device_ids=true | all-gather | bytes 20480 | tf_op jit(solution)/shard_map/all_gather | solution.py:20
  39.3 0.0 copy-done.1
  39.3 0.6 multiply_reduce_fusion.7
  39.9 0.0 copy-start
  39.9 5.6 %fusion.5 = f32[1,1024]{1,0:T(1,128)S(1)} fusion(f32[1024,1]{0,1:T(1,128)S(1)} %bitcast.46, f32[1024,1024]{1,0:T(8,128)} %param.3), kind=kOutput, calls=%fused_computation.23 | convolution fusion | flops 12582912 | bytes 4202496 | tf_op jit(solution)/shard_map/dot_general | solution.py:28
  45.6 12.8 %all-reduce.2 = (f32[1024]{0:T(1024)S(1)}, f32[]{:T(128)}) all-reduce(f32[1024]{0:T(1024)S(1)} %bitcast.39, f32[]{:T(128)} %get-tuple-element.21), channel_id=1, replica_groups=mesh['dp'=4,'feat'=8] {'feat'}, use_global_device_ids=true, to_apply=%region_4.0 | all-reduce | flops 1025 | bytes 8200 | tf_op jit(solution)/shard_map/psum | solution.py:27
  58.3 0.6 multiply_reduce_fusion.6
  58.9 4.3 %fusion.6 = f32[1,1024]{1,0:T(1,128)S(1)} fusion(f32[1024,1]{0,1:T(1,128)S(1)} %bitcast.36, f32[1024,1024]{1,0:T(8,128)} %param.3), kind=kOutput, calls=%fused_computation.24 | convolution fusion | flops 12582912 | bytes 4202496 | tf_op jit(solution)/shard_map/dot_general | solution.py:32
  63.2 12.6 %all-reduce.5 = (f32[1024]{0:T(1024)S(1)}, f32[]{:T(128)}) all-reduce(f32[1024]{0:T(1024)S(1)} %bitcast.40, f32[]{:T(128)} %get-tuple-element.29), channel_id=1, replica_groups=mesh['dp'=4,'feat'=8] {'dp'}, use_global_device_ids=true, to_apply=%region_7.0 | all-reduce | flops 1025 | bytes 8200 | tf_op jit(solution)/shard_map/psum | solution.py:31
  77.7 0.6 multiply_reduce_fusion.5
  78.4 12.6 %psum.113 = f32[]{:T(128)} all-reduce(f32[]{:T(128)} %multiply_reduce_fusion.5), channel_id=1, replica_groups=mesh['dp'=4,'feat'=8] {'feat'}, use_global_device_ids=true, to_apply=%region_9.0 | all-reduce | flops 1 | bytes 8 | tf_op jit(solution)/shard_map/psum | solution.py:12
  92.3 0.6 multiply_reduce_fusion.4
  92.9 5.6 %fusion.7 = f32[1,1024]{1,0:T(1,128)S(1)} fusion(f32[1024,1]{0,1:T(1,128)S(1)} %bitcast.32, f32[1024,1024]{1,0:T(8,128)} %param.3), kind=kOutput, calls=%fused_computation.25 | convolution fusion | flops 12582912 | bytes 4202496 | tf_op jit(solution)/shard_map/dot_general | solution.py:28
  98.5 12.8 %all-reduce.1 = (f32[1024]{0:T(1024)S(1)}, f32[]{:T(128)}) all-reduce(f32[1024]{0:T(1024)S(1)} %bitcast.43, f32[]{:T(128)} %get-tuple-element.19), channel_id=1, replica_groups=mesh['dp'=4,'feat'=8] {'feat'}, use_global_device_ids=true, to_apply=%region_12.0 | all-reduce | flops 1025 | bytes 8200 | tf_op jit(solution)/shard_map/psum | solution.py:27
  111.3 0.7 multiply_reduce_fusion.3
  112.0 4.3 %fusion.8 = f32[1,1024]{1,0:T(1,128)S(1)} fusion(f32[1024,1]{0,1:T(1,128)S(1)} %bitcast.37, f32[1024,1024]{1,0:T(8,128)} %param.3), kind=kOutput, calls=%fused_computation.26 | convolution fusion | flops 12582912 | bytes 4202496 | tf_op jit(solution)/shard_map/dot_general | solution.py:32
  116.2 9.1 %all-reduce.4 = (f32[1024]{0:T(1024)S(1)}, f32[]{:T(128)}) all-reduce(f32[1024]{0:T(1024)S(1)} %bitcast.41, f32[]{:T(128)} %get-tuple-element.27), channel_id=1, replica_groups=mesh['dp'=4,'feat'=8] {'dp'}, use_global_device_ids=true, to_apply=%region_15.0 | all-reduce | flops 1025 | bytes 8200 | tf_op jit(solution)/shard_map/psum | solution.py:31
  127.2 0.6 multiply_reduce_fusion.2
  127.8 12.4 %psum.118 = f32[]{:T(128)} all-reduce(f32[]{:T(128)} %get-tuple-element.17), channel_id=1, replica_groups=mesh['dp'=4,'feat'=8] {'feat'}, use_global_device_ids=true, to_apply=%region_17.0 | all-reduce | flops 1 | bytes 8 | tf_op jit(solution)/shard_map/psum | solution.py:12
  141.6 0.6 multiply_reduce_fusion.1
  142.2 5.6 %fusion.9 = f32[1,1024]{1,0:T(1,128)S(1)} fusion(f32[1024,1]{0,1:T(1,128)S(1)} %bitcast.33, f32[1024,1024]{1,0:T(8,128)} %param.3), kind=kOutput, calls=%fused_computation.27 | convolution fusion | flops 12582912 | bytes 4202496 | tf_op jit(solution)/shard_map/dot_general | solution.py:28
  147.8 12.7 %all-reduce = (f32[]{:T(128)}, f32[1024]{0:T(1024)S(1)}) all-reduce(f32[]{:T(128)} %get-tuple-element.15, f32[1024]{0:T(1024)S(1)} %bitcast.44), channel_id=1, replica_groups=mesh['dp'=4,'feat'=8] {'feat'}, use_global_device_ids=true, to_apply=%region_19.0 | all-reduce | flops 1025 | bytes 8200 | tf_op jit(solution)/shard_map/psum | solution.py:27
  160.6 0.7 fusion
  161.2 4.3 %fusion.10 = f32[1,1024]{1,0:T(1,128)S(1)} fusion(f32[1024,1]{0,1:T(1,128)S(1)} %bitcast.35, f32[1024,1024]{1,0:T(8,128)} %param.3), kind=kOutput, calls=%fused_computation.28 | convolution fusion | flops 12582912 | bytes 4202496 | tf_op jit(solution)/shard_map/dot_general | solution.py:32
  165.5 11.1 %all-reduce.3 = (f32[]{:T(128)}, f32[1024]{0:T(1024)S(1)}) all-reduce(f32[]{:T(128)} %get-tuple-element.26, f32[1024]{0:T(1024)S(1)} %bitcast.42), channel_id=1, replica_groups=mesh['dp'=4,'feat'=8] {'dp'}, use_global_device_ids=true, to_apply=%region_22.0 | all-reduce | flops 1025 | bytes 8200 | tf_op jit(solution)/shard_map/psum | solution.py:31
  178.5 0.0 copy-done
  178.5 0.6 multiply_subtract_fusion
  (4 shorter events, 0.0 us)
Async XLA Ops:
  0.6 20.9 %copy-start.2 = (s32[1024]{0:T(1024)S(1)}, s32[1024]{0:T(1024)}, u32[]{:S(2)}) copy-start(s32[1024]{0:T(1024)} %param.4) | copy-start | bytes 12292
  0.6 38.7 %copy-start.1 = (f32[1024]{0:T(1024)S(1)}, f32[1024]{0:T(1024)}, u32[]{:S(2)}) copy-start(f32[1024]{0:T(1024)} %param.5) | copy-start | bytes 12292
  39.9 138.6 %copy-start = (f32[1024]{0:T(1024)}, f32[1024]{0:T(1024)S(1)}, u32[]{:S(2)}) copy-start(f32[1024]{0:T(1024)S(1)} %get-tuple-element.22) | copy-start | bytes 12292
